TPU v7x, 512 devices: a whole 4x8x8 slice. The times are simulated.
512 devices in a mesh: row: 16 (over x, y_hi, core), col: 32 (over y_lo, z).
Axes of the slice: x: 4, y: 8 (y_hi: 2, y_lo: 4; y = y_hi * 4 + y_lo), z: 8, core: 2. Of those that a mesh axis runs over, the one named last changes fastest.
Arguments:
- resident: float32 [12288, 12288], P('row', 'col')
- factor: float32 [1, 12288, 512], P(None, 'col', 'row'), may hold values from -0.078125 to 0.078125
- dinv: float32 [1, 512, 512], P(None, 'col')
- panel_cols: int32 [1, 512], replicated, may hold values from 0 to 12287, as said below
- row_lists: int32 [1, 6144], replicated, may hold values from 0 to 12287, as said below
Outputs:
- inverse_out: float32 [12288, 12288], P('row', 'col')
Inputs may be any that keep to these rules, and one draw needn't show every extreme that they name: The entries of panel_cols are distinct positions. The resident array and every dinv[k] are symmetric. Each row_lists[k] holds distinct positions, none of them in panel_cols[j] for any j <= k.
All inputs are finite; a program needn't handle non-finite values.
Results may differ from a plain program's by a relative error of at most 0.0001.
Values sent between devices are 32-bit elements; how exact they have to be, the bound alone decides.
No kernel may reach another device: no remote copies, remote signals or barrier semaphores. Data moves between devices by JAX's collectives and lax.ppermute only.
A program may use at most 64 MiB of HBM per device.

v0:
```python
import jax
import jax.numpy as jnp
from jax import lax
from jax.sharding import Mesh
from jax.sharding import PartitionSpec as P

ROW = ("row_0", "row_1", "row_2")


def split_up(shard, dim, count):
    shape = shard.shape
    blocks = shard.reshape(*shape[:dim], count, shape[dim] // count, *shape[dim + 1 :])
    return jnp.moveaxis(blocks, dim, 0)


def sum_at_owner(shard, axis, dim):
    count = lax.axis_size(axis)
    blocks = lax.all_to_all(split_up(shard, dim, count), axis, 0, 0, tiled=True)
    return jnp.sum(blocks, axis=0)


def in_order(blocks, dim):
    shape = list(blocks.shape[1:])
    shape[dim] *= blocks.shape[0]
    return jnp.moveaxis(blocks, 0, dim).reshape(shape)


def sent_to_all(shard, axis):
    copies = jnp.broadcast_to(shard, (lax.axis_size(axis), *shard.shape))
    return lax.all_to_all(copies, axis, split_axis=0, concat_axis=0, tiled=True)


def gathered_copies(shard, axis, dim):
    return in_order(sent_to_all(shard, axis), dim)


def padded_to(lines, count):
    spare = -len(lines) % count
    return jnp.pad(lines, [(0, spare)] + [(0, 0)] * (lines.ndim - 1))


def gather_axes(shard, axes, dim):
    far, near = axes
    initial = sent_to_all(shard, far)
    blocks = jnp.swapaxes(sent_to_all(initial, near), 0, 1)
    return in_order(blocks.reshape(-1, *shard.shape), dim)


def summed_rows(shard, axes, dim):
    far, near = axes
    blocks = split_up(shard, dim, lax.axis_size(far))
    nearer = sum_at_owner(blocks, near, dim + 1)
    arrived = lax.all_to_all(nearer, far, split_axis=0, concat_axis=0, tiled=True)
    return arrived.sum(axis=0)


def sum_by_parts(shard, axes):
    lines = shard.reshape(-1, shard.shape[-1])
    padded = padded_to(lines, lax.axis_size(axes[0]) * lax.axis_size(axes[1]))
    whole = gather_axes(summed_rows(padded, axes, 0), axes, 0)
    return lax.slice_in_dim(whole, 0, len(lines)).reshape(shard.shape)


def sum_by_parts_2(shard, axes):
    lines = shard.reshape(-1, shard.shape[-1])
    own = sum_at_owner(padded_to(lines, lax.axis_size(axes)), axes, 0)
    whole = gathered_copies(own, axes, 0)
    return whole[: len(lines)].reshape(shard.shape)


def on_device(resident, factor, dinv, panel_cols, row_lists):
    highest = lax.Precision.HIGHEST
    row_count = lax.axis_size(ROW)
    col_count = lax.axis_size("col")
    ratio = col_count // row_count
    row_block, col_block = resident.shape
    total = row_block * row_count
    width = panel_cols.shape[1]
    dinv_rows = dinv.shape[1]
    row_pos = lax.axis_index(ROW)
    col_pos = lax.axis_index("col")
    row_ids = row_pos * row_block + jnp.arange(row_block, dtype=jnp.int32)
    col_ids = col_pos * col_block + jnp.arange(col_block, dtype=jnp.int32)
    matrix = resident
    for panel in reversed(range(factor.shape[0])):
        in_rows = jnp.zeros((total,), jnp.float32).at[row_lists[panel]].set(1.0)
        panel_map = (
            jnp.full((total,), -1, jnp.int32)
            .at[panel_cols[panel]]
            .set(jnp.arange(width, dtype=jnp.int32))
        )
        col_mask = in_rows[col_ids]
        gathered = lax.all_gather(factor[panel], ROW, axis=1, tiled=True)
        lower_cols = gathered * col_mask[:, None]
        partial_value = jnp.dot(matrix, lower_cols, precision=highest)
        shares = sum_at_owner(-partial_value, "col", 0)
        product_rows = gathered_copies(shares, "col", 0)
        owner = col_pos // ratio
        offset = col_pos % ratio * col_block
        mine = lax.dynamic_slice_in_dim(product_rows, offset, col_block, 0)
        masked = jnp.where(row_pos == owner, mine, jnp.zeros_like(mine))
        product_cols = sum_by_parts(masked, (("row_0", "row_1"), "row_2"))
        placed = lax.dynamic_update_slice(
            jnp.zeros((width, width), jnp.float32), dinv[panel], (col_pos * dinv_rows, 0)
        )
        gram_term = jnp.dot(lower_cols.T, product_cols, precision=highest)
        diagonal = sum_by_parts_2(placed - gram_term, "col")
        row_slot = panel_map[row_ids]
        col_slot = panel_map[col_ids]
        row_safe = jnp.maximum(row_slot, 0)
        col_safe = jnp.maximum(col_slot, 0)
        row_in = in_rows[row_ids] > 0.5
        col_in = col_mask > 0.5
        row_panel = row_slot >= 0
        col_panel = col_slot >= 0
        below = jnp.take(product_rows, col_safe, axis=1)
        beside = jnp.take(product_cols, row_safe, axis=1).T
        corner = jnp.take(jnp.take(diagonal, row_safe, axis=0), col_safe, axis=1)
        matrix = jnp.where(
            row_panel[:, None] & col_panel[None, :],
            corner,
            jnp.where(
                row_panel[:, None] & col_in[None, :],
                beside,
                jnp.where(row_in[:, None] & col_panel[None, :], below, matrix),
            ),
        )
    return matrix


def solution(mesh):
    finer = Mesh(
        mesh.devices.reshape(4, 2, 2, mesh.shape["col"]), ("row_0", "row_1", "row_2", "col")
    )
    return jax.shard_map(
        on_device,
        mesh=finer,
        in_specs=(P(ROW, "col"), P(None, "col", ROW), P(None, "col", None), P(), P()),
        out_specs=P(ROW, "col"),
        check_vma=False,
    )
```

profile of v0, /device:TPU:16, one launch (start us, length us, event | category | flops | bytes accessed | tf_op | source)
XLA Modules:
  0.0 302.5 jit_solution(6073321219527905925)
XLA Ops:
  0.8 33.7 %all-gather = f32[1,384,512]{1,2,0:T(8,128)S(1)} all-gather(f32[1,384,32]{1,2,0:T(8,128)} %param.8), channel_id=2, replica_groups=mesh['row_0'=4,'row_1'=2,'row_2'=2,'col'=32] {'row_0','row_1','row_2'}, dimensions={2}, use_global_device_ids=true | all-gather | bytes 835584 | tf_op jit(solution)/shard_map/all_gather | solution.py:93
  34.5 23.0 %scatter_custom_fusion.1 = f32[12288]{0:T(1024)S(1)} fusion(s32[6144]{0:T(1024)S(1)} %bitcast.42, f32[6144]{0:T(1024)S(1)} %broadcast.138, f32[]{:T(128)} %constant.105.clone.1), kind=kCustom, calls=%fused_computation.22 | custom fusion | bytes 49156 | tf_op jit(solution)/shard_map/scatter | solution.py:86
  57.5 2.5 gather_fusion.2
  60.1 3.9 %negate_bitcast_fusion = f32[768,512]{0,1:T(8,128)} fusion(f32[768,384]{1,0:T(8,128)S(1)} %copy-done.1, f32[1,384,512]{1,2,0:T(8,128)S(1)} %all-gather, f32[384]{0:T(512)S(1)} %gather_fusion.2), kind=kOutput, calls=%fused_computation.10 | convolution fusion | flops 1812529152 | bytes 3540480 | tf_op jit(solution)/shard_map/dot_general | solution.py:95
  63.9 1.9 copy.26
  65.8 58.1 %all_to_all.40 = f32[32,24,512]{2,1,0:T(8,128)} all-to-all(f32[32,24,512]{2,1,0:T(8,128)S(1)} %bitcast.39), channel_id=1, replica_groups=mesh['row_0'=4,'row_1'=2,'row_2'=2,'col'=32] {'col'}, dimensions={0} | all-to-all | bytes 3145728 | tf_op jit(solution)/shard_map/all_to_all | solution.py:18
  123.9 1.5 reduce_sum.36
  126.8 6.6 %all-to-all-start.1 = ((f32[32,24,512]{2,1,0:T(8,128)}), f32[32,24,512]{2,1,0:T(8,128)S(1)}, u32[]{:S(2)}, u32[]{:S(2)}) async-start(f32[32,24,512]{2,1,0:T(8,128)} %broadcast_in_dim.74), calls=%async_computation.1 | async-start | bytes 3145728 | tf_op jit(solution)/shard_map/all_to_all | solution.py:30
  133.4 39.3 %all-to-all-done.1 = f32[32,24,512]{2,1,0:T(8,128)S(1)} async-done(((f32[32,24,512]{2,1,0:T(8,128)}), f32[32,24,512]{2,1,0:T(8,128)S(1)}, u32[]{:S(2)}, u32[]{:S(2)}) %all-to-all-start.1) | async-done | bytes 1572896 | tf_op jit(solution)/shard_map/all_to_all | solution.py:30
  173.9 4.4 %all_to_all.41 = f32[2,8,24,512]{3,2,1,0:T(8,128)S(1)} all-to-all(f32[2,8,24,512]{3,2,1,0:T(8,128)S(1)} %copy.27), channel_id=1, replica_groups=mesh['row_0'=4,'row_1'=2,'row_2'=2,'col'=32] {'row_2'}, dimensions={0} | all-to-all | bytes 1572864 | tf_op jit(solution)/shard_map/all_to_all | solution.py:18
  178.3 20.3 %all_to_all.42 = f32[8,24,512]{2,1,0:T(8,128)S(1)} all-to-all(f32[8,24,512]{2,1,0:T(8,128)S(1)} %reduce_sum.37), channel_id=1, replica_groups=mesh['row_0'=4,'row_1'=2,'row_2'=2,'col'=32] {'row_0','row_1'}, dimensions={0} | all-to-all | bytes 786432 | tf_op jit(solution)/shard_map/all_to_all | solution.py:53
  199.4 3.5 %all-to-all-start.4 = ((f32[8,24,512]{2,1,0:T(8,128)}), f32[8,24,512]{2,1,0:T(8,128)S(1)}, u32[]{:S(2)}, u32[]{:S(2)}) async-start(f32[8,24,512]{2,1,0:T(8,128)} %broadcast_in_dim.76), calls=%async_computation.4 | async-start | bytes 786432 | tf_op jit(solution)/shard_map/all_to_all | solution.py:30
  203.0 14.7 %all-to-all-done.4 = f32[8,24,512]{2,1,0:T(8,128)S(1)} async-done(((f32[8,24,512]{2,1,0:T(8,128)}), f32[8,24,512]{2,1,0:T(8,128)S(1)}, u32[]{:S(2)}, u32[]{:S(2)}) %all-to-all-start.4) | async-done | bytes 393248 | tf_op jit(solution)/shard_map/all_to_all | solution.py:30
  217.8 4.4 %all_to_all.43 = f32[2,8,24,512]{3,2,1,0:T(8,128)S(1)} all-to-all(f32[2,8,24,512]{3,2,1,0:T(8,128)S(1)} %broadcast_in_dim.77), channel_id=1, replica_groups=mesh['row_0'=4,'row_1'=2,'row_2'=2,'col'=32] {'row_2'}, dimensions={0} | all-to-all | bytes 1572864 | tf_op jit(solution)/shard_map/all_to_all | solution.py:30
  222.2 1.8 convolution_subtract_fusion
  224.1 31.9 %all_to_all.44 = f32[32,16,512]{2,1,0:T(8,128)S(1)} all-to-all(f32[32,16,512]{2,1,0:T(8,128)S(1)} %bitcast.40), channel_id=1, replica_groups=mesh['row_0'=4,'row_1'=2,'row_2'=2,'col'=32] {'col'}, dimensions={0} | all-to-all | bytes 2097152 | tf_op jit(solution)/shard_map/all_to_all | solution.py:18
  257.2 6.0 %all-to-all-start.7 = ((f32[32,16,512]{2,1,0:T(8,128)}), f32[32,16,512]{2,1,0:T(8,128)S(1)}, u32[]{:S(2)}, u32[]{:S(2)}) async-start(f32[32,16,512]{2,1,0:T(8,128)} %broadcast_in_dim.78), calls=%async_computation.7 | async-start | bytes 2097152 | tf_op jit(solution)/shard_map/all_to_all | solution.py:30
  263.3 2.6 scatter_custom_fusion
  265.9 2.5 gather_fusion.1
  268.5 4.5 %gather_fusion = s32[768]{0:T(1024)S(1)} fusion(s32[12288]{0:T(1024)S(1)} %scatter_custom_fusion, s32[1024]{0:T(1024)S(1)} %pad_clamp_fusion.3), kind=kCustom, calls=%fused_computation.2 | custom fusion | bytes 9216 | tf_op jit(solution)/shard_map/gather | solution.py:108
  273.0 4.5 %gather_fusion.5 = f32[768]{0:T(1024)S(1)} fusion(f32[12288]{0:T(1024)S(1)} %scatter_custom_fusion.1, s32[1024]{0:T(1024)S(1)} %pad_clamp_fusion.3), kind=kCustom, calls=%fused_computation.7 | custom fusion | bytes 9216 | tf_op jit(solution)/shard_map/gather | solution.py:112
  277.5 1.4 copy.33
  278.9 1.9 copy.32
  280.8 2.5 gather_fusion.7
  283.6 2.1 gather_fusion.4
  285.7 1.4 copy.31
  287.1 3.7 %all-to-all-done.7 = f32[32,16,512]{2,1,0:T(8,128)S(1)} async-done(((f32[32,16,512]{2,1,0:T(8,128)}), f32[32,16,512]{2,1,0:T(8,128)S(1)}, u32[]{:S(2)}, u32[]{:S(2)}) %all-to-all-start.7) | async-done | bytes 1048608 | tf_op jit(solution)/shard_map/all_to_all | solution.py:30
  290.8 3.1 %gather_fusion.3 = f32[768,512]{1,0:T(8,128)} fusion(f32[512,512]{1,0:T(8,128)S(1)} %bitcast.34, s32[1024]{0:T(1024)S(1)} %pad_clamp_fusion.1), kind=kCustom, calls=%fused_computation.5 | custom fusion | bytes 3148800 | tf_op jit(solution)/shard_map/jit(_take)/gather | solution.py:118
  294.0 1.6 broadcast_select_fusion
  296.0 2.5 gather_fusion.6
  298.5 2.6 fusion.1
  301.1 1.4 copy.34
  (42 shorter events, 6.4 us)
Async XLA Ops:
  34.5 25.6 %copy-start.1 = (f32[768,384]{1,0:T(8,128)S(1)}, f32[768,384]{1,0:T(8,128)}, u32[]{:S(2)}) copy-start(f32[768,384]{1,0:T(8,128)} %param.7) | copy-start | bytes 3538948
  126.8 46.0 %all-to-all-start.1 = ((f32[32,24,512]{2,1,0:T(8,128)}), f32[32,24,512]{2,1,0:T(8,128)S(1)}, u32[]{:S(2)}, u32[]{:S(2)}) async-start(f32[32,24,512]{2,1,0:T(8,128)} %broadcast_in_dim.74), calls=%async_computation.1 | async-start | bytes 3145728 | tf_op jit(solution)/shard_map/all_to_all | solution.py:30
  172.7 1.2 copy-start
  198.6 4.4 %copy-start.4 = (f32[1,16,512]{2,1,0:T(8,128)S(1)}, f32[1,16,512]{2,1,0:T(8,128)}, u32[]{:S(2)}) copy-start(f32[1,16,512]{2,1,0:T(8,128)} %param.9) | copy-start | bytes 98308
  199.4 18.3 %all-to-all-start.4 = ((f32[8,24,512]{2,1,0:T(8,128)}), f32[8,24,512]{2,1,0:T(8,128)S(1)}, u32[]{:S(2)}, u32[]{:S(2)}) async-start(f32[8,24,512]{2,1,0:T(8,128)} %broadcast_in_dim.76), calls=%async_computation.4 | async-start | bytes 786432 | tf_op jit(solution)/shard_map/all_to_all | solution.py:30
  257.2 6.1 %copy-start.5 = (s32[1,512]{1,0:T(1,128)S(1)}, s32[1,512]{1,0:T(1,128)}, u32[]{:S(2)}) copy-start(s32[1,512]{1,0:T(1,128)} %param.10) | copy-start | bytes 6148
  257.2 33.7 %all-to-all-start.7 = ((f32[32,16,512]{2,1,0:T(8,128)}), f32[32,16,512]{2,1,0:T(8,128)S(1)}, u32[]{:S(2)}, u32[]{:S(2)}) async-start(f32[32,16,512]{2,1,0:T(8,128)} %broadcast_in_dim.78), calls=%async_computation.7 | async-start | bytes 2097152 | tf_op jit(solution)/shard_map/all_to_all | solution.py:30
  273.0 4.5 %copy-start.2 = (f32[768,384]{1,0:T(8,128)S(1)}, f32[768,384]{1,0:T(8,128)}, u32[]{:S(2)}) copy-start(f32[768,384]{1,0:T(8,128)} %param.7) | copy-start | bytes 3538948
  296.0 2.5 copy-start.3
where the time goes:
time: 303 us
  blocking collectives  153 us (50%)
  local copies, waits for them, and re-layouts  63.1 us (21%)
  waiting for transfers between devices  57.8 us (19%)
  starting transfers between devices  16.1 us (5%)
  other arithmetic  6.79 us (2%)
  matrix products  5.68 us (2%)
    all_to_all x3, blocking collectives, sum_at_owner(): blocks = lax.all_to_all(split_up(shard, dim, count), axis, 0, 0, tiled=True)  94.4 us
    all_to_all x3, waiting for transfers between devices, sent_to_all(): return lax.all_to_all(copies, axis, split_axis=0, concat_axis=0, tiled=True)  57.8 us
    all_gather x1, blocking collectives, on_device(): gathered = lax.all_gather(factor[panel], ROW, axis=1, tiled=True)  33.7 us
    scatter x1, local copies, waits for them, and re-layouts, on_device(): in_rows = jnp.zeros((total,), jnp.float32).at[row_lists[panel]].set(1.0)  23 us
    all_to_all x1, blocking collectives, summed_rows(): lax.all_to_all(nearer, far, split_axis=0, concat_axis=0, tiled=True)  20.3 us
    all_to_all x3, starting transfers between devices, sent_to_all(): return lax.all_to_all(copies, axis, split_axis=0, concat_axis=0, tiled=True)  16.1 us
  transfers between devices with their start and end apart: 3, of which 3 were waited for; matrix products, arithmetic and copies ran while one was open for 8% of the time, Pallas kernels for 0%

commit v1 on v0

--- a/solution.py
+++ b/solution.py
@@ -90,7 +90,9 @@
             .set(jnp.arange(width, dtype=jnp.int32))
         )
         col_mask = in_rows[col_ids]
-        gathered = lax.all_gather(factor[panel], ROW, axis=1, tiled=True)
+        gathered = jnp.concatenate(
+            lax.all_to_all(jnp.stack([factor[panel]] * lax.axis_size(ROW)), ROW, 0, 0), axis=1
+        )
         lower_cols = gathered * col_mask[:, None]
         partial_value = jnp.dot(matrix, lower_cols, precision=highest)
         shares = sum_at_owner(-partial_value, "col", 0)

time: 303 us -> 278 us (0.917)
  blocking collectives: 153 us -> 121 us
  starting transfers between devices: 16.1 us -> 23.8 us
  local copies, waits for them, and re-layouts: 63.1 us -> 68.4 us
    all_gather x1 -> x0, blocking collectives: 33.7 us -> none  [on_device(): gathered = lax.all_gather(factor[panel], ROW, axis=1, tiled=True)]
    all_to_all x0 -> x1, starting transfers between devices: none -> 7.87 us  [on_device(): lax.all_to_all(jnp.stack([factor[panel]] * lax.axis_size(ROW)), ROW, 0, 0)]
    all_to_all x1, blocking collectives: 20.3 us -> 24.4 us  [summed_rows(): lax.all_to_all(nearer, far, split_axis=0, concat_axis=0, tiled=True)]
    all_to_all x3, waiting for transfers between devices: 57.8 us -> 54.5 us  [sent_to_all(): return lax.all_to_all(copies, axis, split_axis=0, concat_axis=0, tiled=True)]
  transfers between devices with their start and end apart: 3 -> 4, of which waited for: 3 -> 4; matrix products, arithmetic and copies ran while one was open for 8% -> 19% of each run, Pallas kernels for 0% -> 0%
where the time goes in v1:
time: 278 us
  blocking collectives  121 us (44%)
  local copies, waits for them, and re-layouts  68.4 us (25%)
  waiting for transfers between devices  54.8 us (20%)
  starting transfers between devices  23.8 us (9%)
  other arithmetic  4.88 us (2%)
  matrix products  4.51 us (2%)
    all_to_all x3, blocking collectives, sum_at_owner(): blocks = lax.all_to_all(split_up(shard, dim, count), axis, 0, 0, tiled=True)  91.9 us
    all_to_all x3, waiting for transfers between devices, sent_to_all(): return lax.all_to_all(copies, axis, split_axis=0, concat_axis=0, tiled=True)  54.5 us
    all_to_all x1, blocking collectives, summed_rows(): lax.all_to_all(nearer, far, split_axis=0, concat_axis=0, tiled=True)  24.4 us
    scatter x1, local copies, waits for them, and re-layouts, on_device(): in_rows = jnp.zeros((total,), jnp.float32).at[row_lists[panel]].set(1.0)  23 us
    all_to_all x3, starting transfers between devices, sent_to_all(): return lax.all_to_all(copies, axis, split_axis=0, concat_axis=0, tiled=True)  15.9 us
    all_to_all x1, starting transfers between devices, on_device(): lax.all_to_all(jnp.stack([factor[panel]] * lax.axis_size(ROW)), ROW, 0, 0)  7.87 us
    gather x2, local copies, waits for them, and re-layouts, on_device(): beside = jnp.take(product_cols, row_safe, axis=1).T  5.71 us
  transfers between devices with their start and end apart: 4, of which 4 were waited for; matrix products, arithmetic and copies ran while one was open for 19% of the time, Pallas kernels for 0%

profile of v1, /device:TPU:16, one launch (start us, length us, event | category | flops | bytes accessed | tf_op | source)
XLA Modules:
  0.0 277.5 jit_solution(15970481965888000474)
XLA Ops:
  0.0 1.8 stack.3
  1.8 7.9 %all-to-all-start = ((f32[16,384,32]{1,2,0:T(8,128)}), f32[16,384,32]{1,2,0:T(8,128)S(1)}, u32[]{:S(2)}, u32[]{:S(2)}) async-start(f32[16,384,32]{1,2,0:T(8,128)} %stack.3), calls=%async_computation | async-start | bytes 1572864 | tf_op jit(solution)/shard_map/all_to_all | solution.py:94
  9.7 23.0 %scatter_custom_fusion.1 = f32[12288]{0:T(1024)S(1)} fusion(s32[6144]{0:T(1024)S(1)} %bitcast.49, f32[6144]{0:T(1024)S(1)} %broadcast.143, f32[]{:T(128)} %constant.105.clone.1), kind=kCustom, calls=%fused_computation.21 | custom fusion | bytes 49156 | tf_op jit(solution)/shard_map/scatter | solution.py:86
  32.8 2.5 gather_fusion.2
  36.9 2.7 negate_bitcast_fusion
  39.6 1.6 copy.27
  41.2 51.8 %all_to_all.45 = f32[32,24,512]{2,1,0:T(8,128)S(1)} all-to-all(f32[32,24,512]{2,1,0:T(8,128)} %bitcast.44), channel_id=1, replica_groups=mesh['row_0'=4,'row_1'=2,'row_2'=2,'col'=32] {'col'}, dimensions={0} | all-to-all | bytes 3145728 | tf_op jit(solution)/shard_map/all_to_all | solution.py:18
  94.4 6.4 %all-to-all-start.2 = ((f32[32,24,512]{2,1,0:T(8,128)}), f32[32,24,512]{2,1,0:T(8,128)S(1)}, u32[]{:S(2)}, u32[]{:S(2)}) async-start(f32[32,24,512]{2,1,0:T(8,128)} %broadcast_in_dim.74), calls=%async_computation.2 | async-start | bytes 3145728 | tf_op jit(solution)/shard_map/all_to_all | solution.py:30
  100.9 39.0 %all-to-all-done.2 = f32[32,24,512]{2,1,0:T(8,128)S(1)} async-done(((f32[32,24,512]{2,1,0:T(8,128)}), f32[32,24,512]{2,1,0:T(8,128)S(1)}, u32[]{:S(2)}, u32[]{:S(2)}) %all-to-all-start.2) | async-done | bytes 1572896 | tf_op jit(solution)/shard_map/all_to_all | solution.py:30
  141.1 4.4 %all_to_all.46 = f32[2,8,24,512]{3,2,1,0:T(8,128)S(1)} all-to-all(f32[2,8,24,512]{3,2,1,0:T(8,128)S(1)} %copy.28), channel_id=1, replica_groups=mesh['row_0'=4,'row_1'=2,'row_2'=2,'col'=32] {'row_2'}, dimensions={0} | all-to-all | bytes 1572864 | tf_op jit(solution)/shard_map/all_to_all | solution.py:18
  145.5 24.4 %all_to_all.47 = f32[8,24,512]{2,1,0:T(8,128)S(1)} all-to-all(f32[8,24,512]{2,1,0:T(8,128)S(1)} %reduce_sum.37), channel_id=1, replica_groups=mesh['row_0'=4,'row_1'=2,'row_2'=2,'col'=32] {'row_0','row_1'}, dimensions={0} | all-to-all | bytes 786432 | tf_op jit(solution)/shard_map/all_to_all | solution.py:53
  170.7 3.5 %all-to-all-start.5 = ((f32[8,24,512]{2,1,0:T(8,128)}), f32[8,24,512]{2,1,0:T(8,128)S(1)}, u32[]{:S(2)}, u32[]{:S(2)}) async-start(f32[8,24,512]{2,1,0:T(8,128)} %broadcast_in_dim.76), calls=%async_computation.5 | async-start | bytes 786432 | tf_op jit(solution)/shard_map/all_to_all | solution.py:30
  174.4 13.9 %all-to-all-done.5 = f32[8,24,512]{2,1,0:T(8,128)S(1)} async-done(((f32[8,24,512]{2,1,0:T(8,128)}), f32[8,24,512]{2,1,0:T(8,128)S(1)}, u32[]{:S(2)}, u32[]{:S(2)}) %all-to-all-start.5) | async-done | bytes 393248 | tf_op jit(solution)/shard_map/all_to_all | solution.py:30
  188.4 4.4 %all_to_all.48 = f32[2,8,24,512]{3,2,1,0:T(8,128)S(1)} all-to-all(f32[2,8,24,512]{3,2,1,0:T(8,128)S(1)} %broadcast_in_dim.77), channel_id=1, replica_groups=mesh['row_0'=4,'row_1'=2,'row_2'=2,'col'=32] {'row_2'}, dimensions={0} | all-to-all | bytes 1572864 | tf_op jit(solution)/shard_map/all_to_all | solution.py:30
  192.8 1.8 convolution_subtract_fusion
  194.6 35.8 %all_to_all.49 = f32[32,16,512]{2,1,0:T(8,128)S(1)} all-to-all(f32[32,16,512]{2,1,0:T(8,128)S(1)} %bitcast.45), channel_id=1, replica_groups=mesh['row_0'=4,'row_1'=2,'row_2'=2,'col'=32] {'col'}, dimensions={0} | all-to-all | bytes 2097152 | tf_op jit(solution)/shard_map/all_to_all | solution.py:18
  231.6 6.0 %all-to-all-start.8 = ((f32[32,16,512]{2,1,0:T(8,128)}), f32[32,16,512]{2,1,0:T(8,128)S(1)}, u32[]{:S(2)}, u32[]{:S(2)}) async-start(f32[32,16,512]{2,1,0:T(8,128)} %broadcast_in_dim.78), calls=%async_computation.8 | async-start | bytes 2097152 | tf_op jit(solution)/shard_map/all_to_all | solution.py:30
  237.7 2.6 scatter_custom_fusion
  240.4 2.5 gather_fusion.1
  243.0 4.5 %gather_fusion = s32[768]{0:T(1024)S(1)} fusion(s32[12288]{0:T(1024)S(1)} %scatter_custom_fusion, s32[1024]{0:T(1024)S(1)} %pad_clamp_fusion.3), kind=kCustom, calls=%fused_computation.2 | custom fusion | bytes 9216 | tf_op jit(solution)/shard_map/gather | solution.py:110
  247.4 4.5 %gather_fusion.5 = f32[768]{0:T(1024)S(1)} fusion(f32[12288]{0:T(1024)S(1)} %scatter_custom_fusion.1, s32[1024]{0:T(1024)S(1)} %pad_clamp_fusion.3), kind=kCustom, calls=%fused_computation.7 | custom fusion | bytes 9216 | tf_op jit(solution)/shard_map/gather | solution.py:114
  251.9 1.4 copy.34
  253.4 1.9 copy.33
  255.3 2.5 gather_fusion.7
  258.0 3.0 %gather_fusion.4 = f32[768,384]{1,0:T(8,128)} fusion(f32[384,512]{0,1:T(8,128)S(1)} %copy.31, s32[1024]{0:T(1024)S(1)} %pad_clamp_fusion.1), kind=kCustom, calls=%fused_computation.6 | custom fusion | bytes 2362368 | tf_op jit(solution)/shard_map/jit(_take)/gather | solution.py:119
  261.0 2.7 copy.32
  263.7 1.6 all-to-all-done.8
  265.3 2.1 gather_fusion.3
  268.8 1.9 copy.30
  270.7 2.5 gather_fusion.6
  273.1 3.0 %fusion.1 = f32[768,384]{0,1:T(8,128)S(1)} fusion(f32[768,384]{0,1:T(8,128)} %copy.34, f32[384,768]{1,0:T(8,128)} %gather_fusion.7, f32[384,768]{1,0:T(8,128)} %gather_fusion.6, f32[768,384]{0,1:T(8,128)} %copy.32, pred[384]{0:T(512)(128)(4,1)S(1)} %get-tuple-element.9, pred[768]{0:T(1024)(128)(4,1)S(1)} %get-tuple-element.7, ...), kind=kLoop, calls=%fused_computation.14 | loop fusion | flops 2654208 | bytes 5901696 | tf_op jit(solution)/shard_map/jit(_where)/select_n | solution.py:121
  276.1 1.4 copy.35
  (46 shorter events, 8.3 us)
Async XLA Ops:
  0.0 9.6 %copy-start.4 = (s32[1,6144]{1,0:T(1,128)S(1)}, s32[1,6144]{1,0:T(1,128)}, u32[]{:S(2)}) copy-start(s32[1,6144]{1,0:T(1,128)} %param.11) | copy-start | bytes 73732
  1.8 33.8 %all-to-all-start = ((f32[16,384,32]{1,2,0:T(8,128)}), f32[16,384,32]{1,2,0:T(8,128)S(1)}, u32[]{:S(2)}, u32[]{:S(2)}) async-start(f32[16,384,32]{1,2,0:T(8,128)} %stack.3), calls=%async_computation | async-start | bytes 1572864 | tf_op jit(solution)/shard_map/all_to_all | solution.py:94
  35.6 1.3 copy-start.1
  94.4 45.5 %all-to-all-start.2 = ((f32[32,24,512]{2,1,0:T(8,128)}), f32[32,24,512]{2,1,0:T(8,128)S(1)}, u32[]{:S(2)}, u32[]{:S(2)}) async-start(f32[32,24,512]{2,1,0:T(8,128)} %broadcast_in_dim.74), calls=%async_computation.2 | async-start | bytes 3145728 | tf_op jit(solution)/shard_map/all_to_all | solution.py:30
  139.9 1.2 copy-start
  169.9 4.4 %copy-start.3 = (f32[1,16,512]{2,1,0:T(8,128)S(1)}, f32[1,16,512]{2,1,0:T(8,128)}, u32[]{:S(2)}) copy-start(f32[1,16,512]{2,1,0:T(8,128)} %param.9) | copy-start | bytes 98308
  170.7 17.6 %all-to-all-start.5 = ((f32[8,24,512]{2,1,0:T(8,128)}), f32[8,24,512]{2,1,0:T(8,128)S(1)}, u32[]{:S(2)}, u32[]{:S(2)}) async-start(f32[8,24,512]{2,1,0:T(8,128)} %broadcast_in_dim.76), calls=%async_computation.5 | async-start | bytes 786432 | tf_op jit(solution)/shard_map/all_to_all | solution.py:30
  231.6 6.1 %copy-start.5 = (s32[1,512]{1,0:T(1,128)S(1)}, s32[1,512]{1,0:T(1,128)}, u32[]{:S(2)}) copy-start(s32[1,512]{1,0:T(1,128)} %param.10) | copy-start | bytes 6148
  231.6 33.7 %all-to-all-start.8 = ((f32[32,16,512]{2,1,0:T(8,128)}), f32[32,16,512]{2,1,0:T(8,128)S(1)}, u32[]{:S(2)}, u32[]{:S(2)}) async-start(f32[32,16,512]{2,1,0:T(8,128)} %broadcast_in_dim.78), calls=%async_computation.8 | async-start | bytes 2097152 | tf_op jit(solution)/shard_map/all_to_all | solution.py:30
  247.4 4.5 %copy-start.2 = (f32[768,384]{1,0:T(8,128)S(1)}, f32[768,384]{1,0:T(8,128)}, u32[]{:S(2)}) copy-start(f32[768,384]{1,0:T(8,128)} %param.7) | copy-start | bytes 3538948
